TPU v7x, 128 devices: a whole 4x4x4 slice. The times are simulated.
128 devices in a mesh: dp: 32 (over x, z, core), expert: 4 (over y).
Axes of the slice: x: 4, y: 4, z: 4, core: 2. Of those that a mesh axis runs over, the one named last changes fastest.
Arguments:
- tokens: bfloat16 [8192, 2048], P('dp'), may hold values from -6 to 6
- routes: int32 [8192, 6], P('dp'), may hold values from 0 to 63, all different within a row; in each aligned block of 256 rows (0 to 255, 256 to 511, ...) at most 32 rows name the same one
- gates: float32 [8192, 6], P('dp'), may hold values from 0.1 to 1
- w_gate: bfloat16 [64, 2048, 1408], P('dp', None, 'expert'), may hold values from -0.125 to 0.125
- w_up: bfloat16 [64, 2048, 1408], P('dp', None, 'expert'), may hold values from -0.125 to 0.125
- w_down: bfloat16 [64, 1408, 2048], P('dp', 'expert'), may hold values from -0.21875 to 0.21875
- s_gate: bfloat16 [2048, 2816], P(None, 'expert'), may hold values from -0.125 to 0.125
- s_up: bfloat16 [2048, 2816], P(None, 'expert'), may hold values from -0.125 to 0.125
- s_down: bfloat16 [2816, 2048], P('expert'), may hold values from -0.15625 to 0.15625
Outputs:
- mixed: bfloat16 [8192, 2048], P('dp', 'expert')
Inputs may be any that keep to these rules, and one draw needn't show every extreme that they name: `routes`: each row names 6 different experts. Within each aligned block of 256 rows (the rows of one index of dp) no expert is named by more than 32 rows; some expert is named by exactly 32 rows in some block of every draw.
All inputs are finite; a program needn't handle non-finite values.
Results may differ from a plain program's by a relative error of at most 0.013.
Values may be sent and summed in bfloat16 or wider, within the bound.
A program may use at most 128 MiB of HBM per device.

v0:
```python
import jax
import jax.numpy as jnp
from jax import lax
from jax.sharding import PartitionSpec as P

CAP = 32


def items_in_groups(array, axis, split_dim, concat_dim, work, item_dim, out_dim):
    items = jax.tree.leaves(array)[0].shape[item_dim]
    count = 2 if items % 2 == 0 else 1
    finished = []
    for k in range(count):
        group = jax.tree.map(
            lambda a: lax.slice_in_dim(
                a, k * (items // count), (k + 1) * (items // count), axis=item_dim
            ),
            array,
        )
        finished.append(
            work(
                lax.all_to_all(
                    group, axis, split_axis=split_dim, concat_axis=concat_dim, tiled=True
                )
            )
        )
    return jax.tree.map(lambda *parts: jnp.concatenate(parts, axis=out_dim), *finished)


def body(tokens, routes, gates, w_gate, w_up, w_down, s_gate, s_up, s_down):
    tok_rows, width = tokens.shape
    local_experts = w_gate.shape[0]
    groups = lax.axis_size("dp")
    members = lax.axis_size("expert")
    experts_all = local_experts * groups
    top_count = routes.shape[1]
    capacity = CAP
    quarter = width // members
    labels = jnp.arange(experts_all, dtype=jnp.int32)
    matches = (routes[:, :, None] == labels[None, None, :]).astype(jnp.int32)
    counts = jnp.sum(matches, axis=1)
    before = jnp.cumsum(counts, axis=0) - counts
    slots = jnp.sum(matches * before[:, None, :], axis=2)
    dest = routes * capacity + slots
    token_ids = jnp.repeat(jnp.arange(tok_rows, dtype=jnp.int32), top_count)
    sources = (
        jnp.full((experts_all * capacity,), tok_rows, jnp.int32).at[dest.reshape(-1)].set(token_ids)
    )
    padded = jnp.concatenate([tokens, jnp.zeros((1, width), tokens.dtype)], axis=0)
    outgoing = padded[sources].reshape(groups, local_experts, capacity, width)

    def expert_work(received):
        gate = jnp.einsum("sjcd,jdf->sjcf", received, w_gate, preferred_element_type=jnp.float32)
        up = jnp.einsum("sjcd,jdf->sjcf", received, w_up, preferred_element_type=jnp.float32)
        hidden = (jax.nn.silu(gate) * up).astype(jnp.bfloat16)
        partial_value = jnp.einsum(
            "sjcf,jfd->sjcd", hidden, w_down, preferred_element_type=jnp.float32
        )
        summed = lax.psum_scatter(
            partial_value.astype(jnp.bfloat16), "expert", scatter_dimension=3, tiled=True
        )
        return lax.all_to_all(summed, "dp", split_axis=0, concat_axis=0, tiled=True)

    returned = items_in_groups(outgoing, "dp", 0, 0, expert_work, 2, 2)
    flat = returned.reshape(experts_all * capacity, quarter)
    picked = flat[dest].astype(jnp.float32)
    routed = jnp.einsum("tk,tkd->td", gates, picked)
    shared_gate = jnp.dot(tokens, s_gate, preferred_element_type=jnp.float32)
    shared_up = jnp.dot(tokens, s_up, preferred_element_type=jnp.float32)
    shared_hidden = (jax.nn.silu(shared_gate) * shared_up).astype(jnp.bfloat16)
    shared_part = jnp.dot(shared_hidden, s_down, preferred_element_type=jnp.float32)
    shared_out = lax.psum_scatter(
        shared_part.astype(jnp.bfloat16), "expert", scatter_dimension=1, tiled=True
    ).astype(jnp.float32)
    return (shared_out + routed).astype(jnp.bfloat16)


def solution(mesh):
    placed = (
        P("dp", None),
        P("dp", None),
        P("dp", None),
        P("dp", None, "expert"),
        P("dp", None, "expert"),
        P("dp", "expert", None),
        P(None, "expert"),
        P(None, "expert"),
        P("expert", None),
    )
    return jax.shard_map(
        body, mesh=mesh, in_specs=placed, out_specs=P("dp", "expert"), check_vma=False
    )
```

profile of v0, /device:TPU:2, one launch (start us, length us, event | category | flops | bytes accessed | tf_op | source)
XLA Modules:
  0.0 277.5 jit_solution(15392993210649181161)
XLA Ops:
  6.5 0.0 copy-start
  6.5 0.0 reduce-scatter.6.cloned.1.call-start
  6.5 0.9 convert_reduce_fusion
  7.5 0.6 reduce-window.6
  8.1 0.2 slice_reduce_fusion
  8.3 0.1 fusion.43
  8.4 0.8 select_reduce_fusion
  9.1 0.7 compare_select_fusion.1
  9.9 0.1 copy.34
  10.0 0.1 reshape.54
  10.2 0.1 reshape.78
  10.3 6.2 %scatter_custom_fusion = s32[2048]{0:T(1024)S(1)} fusion(s32[1536]{0:T(1024)S(1)} %fusion.45, s32[1536]{0:T(1024)S(1)} %reshape.78, s32[]{:T(128)} %constant.9.clone.1), kind=kCustom, calls=%fused_computation.57 | custom fusion | bytes 8196 | tf_op jit(solution)/shard_map/scatter | solution.py:47
  16.5 2.4 concatenate.6
  19.0 17.7 %gather_fusion = bf16[2048,2048]{1,0:T(8,128)(2,1)} fusion(bf16[257,2048]{1,0:T(8,128)(2,1)} %concatenate.6, s32[2048]{0:T(1024)S(1)} %fusion.44), kind=kCustom, calls=%fused_computation | custom fusion | bytes 16785408 | tf_op jit(solution)/shard_map/gather | solution.py:50
  36.7 5.3 %fusion.51 = (bf16[32,2,16,2048]{3,2,1,0:T(8,128)(2,1)S(1)}, bf16[32,2,16,2048]{3,2,1,0:T(8,128)(2,1)}) fusion(bf16[32,2,32,2048]{3,2,1,0:T(8,128)(2,1)} %bitcast.107), kind=kLoop, calls=%fused_computation.62 | loop fusion | bytes 16777216 | tf_op jit(solution)/shard_map/slice | solution.py:15
  42.0 0.0 copy-start.4
  42.0 56.6 %all_to_all.20 = bf16[32,2,16,2048]{3,2,1,0:T(8,128)(2,1)S(1)} all-to-all(bf16[32,2,16,2048]{3,2,1,0:T(8,128)(2,1)S(1)} %get-tuple-element.7), channel_id=1, replica_groups=mesh['dp'=32,'expert'=4] {'dp'}, dimensions={0} | all-to-all | bytes 8388608 | tf_op jit(solution)/shard_map/all_to_all | solution.py:22
  98.6 0.0 copy-start.1
  98.6 1.9 copy-done.1
  100.5 0.0 copy-done.4
  100.5 3.5 %fusion.6 = f32[2,32,16,352]{3,2,1,0:T(8,128)} fusion(bf16[32,2,16,2048]{3,2,1,0:T(8,128)(2,1)S(1)} %all_to_all.20, bf16[2,2048,352]{1,2,0:T(8,128)(2,1)S(1)} %copy-done.4), kind=kOutput, calls=%fused_computation.11 | convolution fusion | flops 1476395008 | bytes 8519680 | tf_op jit(solution)/shard_map/sjcd,jdf->sjcf/dot_general | solution.py:53
  104.1 0.0 copy-done
  104.1 8.3 %convert_bitcast_fusion.1 = bf16[32,2,16,2048]{3,2,0,1:T(8,128)(2,1)} fusion(bf16[2,352,2048]{2,1,0:T(8,128)(2,1)S(1)} %copy-done, f32[2,32,16,352]{3,2,1,0:T(8,128)} %fusion.6, bf16[2,2048,352]{1,2,0:T(8,128)(2,1)} %param.13, bf16[32,2,16,2048]{3,2,1,0:T(8,128)(2,1)} %copy-done.1), kind=kOutput, calls=%fused_computation.4 | convolution fusion | flops 2957049856 | bytes 15597568 | tf_op jit(solution)/shard_map/sjcf,jfd->sjcd/dot_general | solution.py:56
  112.4 0.0 reduce-scatter.6.cloned.1.call-update
  112.4 0.0 reduce-scatter.8.cloned.1.call-start
  112.4 0.0 copy-start.5
  112.5 54.8 %all_to_all.21 = bf16[32,2,16,2048]{3,2,1,0:T(8,128)(2,1)S(1)} all-to-all(bf16[32,2,16,2048]{3,2,1,0:T(8,128)(2,1)} %get-tuple-element.8), channel_id=1, replica_groups=mesh['dp'=32,'expert'=4] {'dp'}, dimensions={0} | all-to-all | bytes 8388608 | tf_op jit(solution)/shard_map/all_to_all | solution.py:22
  167.3 0.0 copy-start.2
  167.3 2.0 copy-done.2
  169.3 0.0 copy-done.5
  169.3 3.5 %fusion.2 = f32[2,32,16,352]{3,2,1,0:T(8,128)} fusion(bf16[32,2,16,2048]{3,2,1,0:T(8,128)(2,1)S(1)} %all_to_all.21, bf16[2,2048,352]{1,2,0:T(8,128)(2,1)S(1)} %copy-done.5), kind=kOutput, calls=%fused_computation.7 | convolution fusion | flops 1476395008 | bytes 8519680 | tf_op jit(solution)/shard_map/sjcd,jdf->sjcf/dot_general | solution.py:53
  172.8 8.2 %convert_bitcast_fusion = bf16[32,2,16,2048]{3,2,0,1:T(8,128)(2,1)} fusion(bf16[2,352,2048]{2,1,0:T(8,128)(2,1)S(1)} %copy-done, f32[2,32,16,352]{3,2,1,0:T(8,128)} %fusion.2, bf16[2,2048,352]{1,2,0:T(8,128)(2,1)} %param.13, bf16[32,2,16,2048]{3,2,1,0:T(8,128)(2,1)} %copy-done.2), kind=kOutput, calls=%fused_computation.3 | convolution fusion | flops 2957049856 | bytes 15597568 | tf_op jit(solution)/shard_map/sjcf,jfd->sjcd/dot_general | solution.py:56
  181.0 0.0 reduce-scatter.8.cloned.1.call-update
  181.1 4.0 %fusion.52 = f32[256,704]{0,1:T(8,128)} fusion(bf16[256,2048]{1,0:T(8,128)(2,1)} %param.9, bf16[2048,704]{0,1:T(8,128)(2,1)} %param.15), kind=kOutput, calls=%fused_computation.63 | convolution fusion | flops 738197504 | bytes 4653056 | tf_op jit(solution)/shard_map/dot_general | solution.py:68
  185.0 0.0 reduce-scatter.6.cloned.1.call-done
  185.0 2.3 copy.37
  187.3 6.9 %all-to-all-start.1 = ((bf16[32,2,16,512]{3,2,1,0:T(8,128)(2,1)}), bf16[32,2,16,512]{3,2,1,0:T(8,128)(2,1)}, u32[]{:S(2)}, u32[]{:S(2)}) async-start(bf16[32,2,16,512]{3,2,1,0:T(8,128)(2,1)} %copy.37), calls=%async_computation.3 | async-start | bytes 2097152 | tf_op jit(solution)/shard_map/all_to_all | solution.py:62
  194.2 0.0 reduce-scatter.4.cloned.1.call-start
  194.3 7.5 %convolution_convert_fusion = bf16[256,2048]{1,0:T(8,128)(2,1)} fusion(bf16[704,2048]{1,0:T(8,128)(2,1)} %param.17, bf16[256,2048]{1,0:T(8,128)(2,1)} %param.9, bf16[2048,704]{0,1:T(8,128)(2,1)} %param.16, f32[256,704]{0,1:T(8,128)} %fusion.52), kind=kOutput, calls=%fused_computation.19 | convolution fusion | flops 1478000640 | bytes 8585216 | tf_op jit(solution)/shard_map/dot_general | solution.py:71
  201.8 0.0 copy-start.3
  201.8 0.0 reduce-scatter.4.cloned.1.call-update
  201.8 26.5 %reduce-scatter.8.cloned.1.call-done = bf16[32,2,16,512]{3,2,0,1:T(8,128)(2,1)} async-done(((bf16[32,2,16,2048]{3,2,0,1:T(8,128)(2,1)}), bf16[32,2,16,512]{3,2,0,1:T(8,128)(2,1)}) %reduce-scatter.8.cloned.1.call-update) | async-done | bytes 1048592 | tf_op jit(solution)/shard_map/reduce_scatter | solution.py:59
  228.4 2.3 copy.40
  230.7 0.0 all-to-all-done.1
  230.7 7.6 %all-to-all-start.3 = ((bf16[32,2,16,512]{3,2,1,0:T(8,128)(2,1)}), bf16[32,2,16,512]{3,2,1,0:T(8,128)(2,1)}, u32[]{:S(2)}, u32[]{:S(2)}) async-start(bf16[32,2,16,512]{3,2,1,0:T(8,128)(2,1)} %copy.40), calls=%async_computation.6 | async-start | bytes 2097152 | tf_op jit(solution)/shard_map/all_to_all | solution.py:62
  238.3 0.1 copy.41
  238.4 0.1 reshape.68
  238.6 0.0 copy-done.3
  238.6 0.2 copy.45
  238.8 14.0 %all-to-all-done.3 = bf16[32,2,16,512]{3,2,1,0:T(8,128)(2,1)} async-done(((bf16[32,2,16,512]{3,2,1,0:T(8,128)(2,1)}), bf16[32,2,16,512]{3,2,1,0:T(8,128)(2,1)}, u32[]{:S(2)}, u32[]{:S(2)}) %all-to-all-start.3) | async-done | bytes 1048608 | tf_op jit(solution)/shard_map/all_to_all | solution.py:62
  252.7 3.1 %pad_maximum_fusion = bf16[32,2,32,512]{3,2,1,0:T(8,128)(2,1)} fusion(bf16[32,2,16,512]{3,2,1,0:T(8,128)(2,1)} %all-to-all-done.3, bf16[32,2,16,512]{3,2,1,0:T(8,128)(2,1)} %all-to-all-done.1), kind=kLoop, calls=%fused_computation.20 | loop fusion | flops 4194304 | bytes 4194304 | tf_op jit(solution)/shard_map/concatenate | solution.py:27
  255.9 7.4 %gather_fusion.1 = bf16[1536,512]{1,0:T(8,128)(2,1)} fusion(bf16[2048,512]{1,0:T(8,128)(2,1)} %bitcast.106, s32[2048]{0:T(1024)S(1)} %pad_clamp_fusion), kind=kCustom, calls=%fused_computation.1 | custom fusion | bytes 3151872 | tf_op jit(solution)/shard_map/gather | solution.py:66
  263.2 3.7 %reshape.67 = bf16[256,6,512]{2,1,0:T(8,128)(2,1)} reshape(bf16[1536,512]{1,0:T(8,128)(2,1)} %gather_fusion.1) | data formatting | bytes 3145728 | tf_op jit(solution)/shard_map/gather | solution.py:66
  266.9 2.3 fusion.53
  269.2 0.0 reduce-scatter.4.cloned.1.call-done
  269.3 1.7 fusion.41
  (7 shorter events, 0.1 us)
Async XLA Ops:
  6.5 97.5 %copy-start = (bf16[2,352,2048]{2,1,0:T(8,128)(2,1)S(1)}, bf16[2,352,2048]{2,1,0:T(8,128)(2,1)}, u32[]{:S(2)}) copy-start(bf16[2,352,2048]{2,1,0:T(8,128)(2,1)} %param.14) | copy-start | bytes 8650756
  6.5 178.5 %reduce-scatter.6.cloned.1.call-start = ((), (), s32[]{:S(2)}) async-start(), calls=%async_computation.8 | async-start | bytes 5242880 | tf_op jit(solution)/shard_map/reduce_scatter | solution.py:59
  42.0 58.6 %copy-start.4 = (bf16[2,2048,352]{1,2,0:T(8,128)(2,1)S(1)}, bf16[2,2048,352]{1,2,0:T(8,128)(2,1)}, u32[]{:S(2)}) copy-start(bf16[2,2048,352]{1,2,0:T(8,128)(2,1)} %param.12) | copy-start | bytes 8650756
  98.6 1.9 copy-start.1
  112.4 116.0 %reduce-scatter.8.cloned.1.call-start = ((), (), s32[]{:S(2)}) async-start(), calls=%async_computation.9 | async-start | bytes 5242880 | tf_op jit(solution)/shard_map/reduce_scatter | solution.py:59
  112.4 56.8 %copy-start.5 = (bf16[2,2048,352]{1,2,0:T(8,128)(2,1)S(1)}, bf16[2,2048,352]{1,2,0:T(8,128)(2,1)}, u32[]{:S(2)}) copy-start(bf16[2,2048,352]{1,2,0:T(8,128)(2,1)} %param.12) | copy-start | bytes 8650756
  167.3 2.0 copy-start.2
  187.3 43.3 %all-to-all-start.1 = ((bf16[32,2,16,512]{3,2,1,0:T(8,128)(2,1)}), bf16[32,2,16,512]{3,2,1,0:T(8,128)(2,1)}, u32[]{:S(2)}, u32[]{:S(2)}) async-start(bf16[32,2,16,512]{3,2,1,0:T(8,128)(2,1)} %copy.37), calls=%async_computation.3 | async-start | bytes 2097152 | tf_op jit(solution)/shard_map/all_to_all | solution.py:62
  194.2 75.0 %reduce-scatter.4.cloned.1.call-start = ((), (), s32[]{:S(2)}) async-start(), calls=%async_computation.7 | async-start | bytes 1310720 | tf_op jit(solution)/shard_map/reduce_scatter | solution.py:72
  201.8 36.8 %copy-start.3 = (f32[256,6]{0,1:T(8,128)S(1)}, f32[256,6]{0,1:T(8,128)}, u32[]{:S(2)}) copy-start(f32[256,6]{0,1:T(8,128)} %param.11) | copy-start | bytes 18436
  230.7 22.1 %all-to-all-start.3 = ((bf16[32,2,16,512]{3,2,1,0:T(8,128)(2,1)}), bf16[32,2,16,512]{3,2,1,0:T(8,128)(2,1)}, u32[]{:S(2)}, u32[]{:S(2)}) async-start(bf16[32,2,16,512]{3,2,1,0:T(8,128)(2,1)} %copy.40), calls=%async_computation.6 | async-start | bytes 2097152 | tf_op jit(solution)/shard_map/all_to_all | solution.py:62
Sparse Core Ops, SparseCore 0:
  112.5 47.1 reduce-scatter.5
  181.2 47.1 reduce-scatter.7
  230.8 23.4 reduce-scatter.3
where the time goes:
time: 282 us; the launch traced here: 278 us
  blocking collectives  111 us (39%)
  local copies, waits for them, and re-layouts  52.3 us (19%)
  waiting for transfers between devices  40.6 us (14%)
  matrix products  37.3 us (13%)
  starting transfers between devices  14.6 us (5%)
  between operations  13.3 us (5%)
  other arithmetic  8 us (3%)
    all_to_all x2, blocking collectives, items_in_groups(): lax.all_to_all(group, axis, split_axis=split_dim, concat_axis=concat_dim,...  111 us
    reduce_scatter x2, waiting for transfers between devices, expert_work(): lax.psum_scatter(partial_value.astype(jnp.bfloat16), 'expert', scatter_di...  26.5 us
    gather x1, local copies, waits for them, and re-layouts, body(): outgoing = padded[sources].reshape(groups, local_experts, capacity, width)  17.7 us
    dot_general x2, matrix products, expert_work(): jnp.einsum('sjcf,jfd->sjcd', hidden, w_down, preferred_element_type=jnp.f...  16.5 us
    all_to_all x2, starting transfers between devices, expert_work(): return lax.all_to_all(summed, 'dp', split_axis=0, concat_axis=0, tiled=True)  14.5 us
    all_to_all x2, waiting for transfers between devices, expert_work(): return lax.all_to_all(summed, 'dp', split_axis=0, concat_axis=0, tiled=True)  14 us
    gather x2, local copies, waits for them, and re-layouts, body(): picked = flat[dest].astype(jnp.float32)  11.1 us
    dot_general x1, matrix products, body(): jnp.dot(shared_hidden, s_down, preferred_element_type=jnp.float32)  7.5 us
  transfers between devices with their start and end apart: 5, of which 2 were waited for; matrix products, arithmetic and copies ran while one was open for 16% of the time, Pallas kernels for 0%

commit v1 on v0

v1 whole, which is shorter than its diff:
```python
import jax
import jax.numpy as jnp
from jax import lax
from jax.experimental import pallas as pl
from jax.experimental.pallas import tpu as pltpu
from jax.sharding import PartitionSpec as P

MESH = pl.DeviceIdType.MESH
BF16 = jnp.bfloat16
F32 = jnp.float32
CAP = 32
CHUNK = 512
WHOLE = (0, 1)
SPLIT = (3, 2)


def dot(a, b):
    return jnp.dot(a, b, preferred_element_type=F32)


def silu(v):
    return v / (1.0 + jnp.exp(-v))


def kernel(
    tok, routes_t, gates_t, wg_h, wu_h, wd_h, sg_h, su_h, sd_h, out,
    info, xinfo, xbuf, slots, zst_a, zst_s, zst_b, ybuf, ysum, zr_a, zr_s, zr_b, xr, acc, y2s, y2r,
    pick, hid, shid, wg, wu, wd, sg, su, sd,
    sx, rx, si, ri, sz, rz, sy, ry, szr, rzr, syr, ryr, sxr, rxr, sy2, ry2, wsem,
):
    me = lax.axis_index("dp")
    y = lax.axis_index("expert")
    x = lax.div(me, 8)
    z = lax.rem(lax.div(me, 2), 4)
    c = lax.rem(me, 2)
    width = tok.shape[1]
    chunks = width // CHUNK

    def at_x(d):
        return {"dp": lax.rem(x + d + 4, 4) * 8 + z * 2 + c}

    def core_of(cc):
        return c if cc == 0 else 1 - c

    def at_z(d, cc):
        return {"dp": x * 8 + lax.rem(z + d + 4, 4) * 2 + core_of(cc)}

    def at_y(p):
        return {"expert": lax.rem(y + p, 4)}

    def remote(src, dst, s, r, where):
        return pltpu.make_async_remote_copy(
            src_ref=src, dst_ref=dst, send_sem=s, recv_sem=r, device_id=where, device_id_type=MESH
        )

    peers = [at_x(d) for d in (1, 2, 3)]
    peers += [at_z(r // 2, r % 2) for r in range(1, 8)]
    peers += [at_y(p) for p in (1, 2, 3)]
    barrier = pltpu.get_barrier_semaphore()
    for peer in peers:
        pl.semaphore_signal(barrier, inc=1, device_id=peer, device_id_type=MESH)
    loads = [
        pltpu.make_async_copy(src, dst, wsem.at[i])
        for i, (src, dst) in enumerate(
            ((sg_h, sg), (su_h, su), (sd_h, sd), (wg_h, wg), (wu_h, wu), (wd_h, wd))
        )
    ]
    for load in loads:
        load.start()
    pl.semaphore_wait(barrier, len(peers))

    near = {
        1: remote(tok, xbuf.at[0], sx.at[0], rx.at[0], at_x(-1)),
        3: remote(tok, xbuf.at[2], sx.at[1], rx.at[1], at_x(1)),
    }
    near[1].start()
    near[3].start()
    half = tok.shape[0] // 2
    relay = {
        1: remote(
            xbuf.at[0, pl.ds(0, half)], xbuf.at[1, pl.ds(0, half)], sx.at[2], rx.at[2], at_x(-1)
        ),
        3: remote(
            xbuf.at[2, pl.ds(half, half)], xbuf.at[1, pl.ds(half, half)], sx.at[3], rx.at[3], at_x(1)
        ),
    }

    rt = routes_t[...]
    rows = tok.shape[0]
    label = lax.broadcasted_iota(jnp.int32, (64, rows), 0)
    hits = jnp.zeros((64, rows), F32)
    for k in range(6):
        hits = hits + jnp.where(rt[k : k + 1, :] == label, 1.0, 0.0)
    earlier = jnp.where(
        lax.broadcasted_iota(jnp.int32, (rows, rows), 0)
        < lax.broadcasted_iota(jnp.int32, (rows, rows), 1),
        1.0,
        0.0,
    )
    before = dot(hits.astype(BF16), earlier.astype(BF16))
    info[...] = jnp.full(info.shape, -1.0, F32)
    for k in range(6):
        slot = jnp.sum(jnp.where(rt[k : k + 1, :] == label, before, 0.0), axis=0, keepdims=True)
        info[k : k + 1, :] = rt[k : k + 1, :].astype(F32) * CAP + slot
        info[8 + k : 9 + k, :] = gates_t[k : k + 1, :]
    tell = {
        j: remote(info, xinfo.at[j - 1], si.at[j - 1], ri.at[j - 1], at_x(-j)) for j in (1, 2, 3)
    }
    for j in (1, 3, 2):
        tell[j].start()

    def base_of(r):
        return (x * 8 + lax.rem(z + r // 2, 4) * 2 + core_of(r % 2)) * 64

    def select(table, base, count, at, weighted):
        ids = (lax.broadcasted_iota(jnp.int32, (count, rows), 0) + base).astype(F32)
        value = jnp.zeros((count, rows), F32)
        for k in range(6):
            given = table[8 + k : 9 + k, :] if weighted else 1.0
            value = value + jnp.where(ids == table[k : k + 1, :], given, 0.0)
        pick[at : at + count, :] = value.astype(BF16)

    def select_whole(table, weighted):
        for r in range(8):
            select(table, base_of(r), 64, r * 64, weighted)

    def select_split(table, weighted):
        for r in range(2):
            select(table, base_of(r), 64, r * 64, weighted)
        for r in range(2, 8):
            select(table, base_of(r) + 16 * y, 16, 128 + (r - 2) * 16, weighted)

    e_y, h_y = lax.div(y, 2), pl.multiple_of(lax.rem(y, 2) * 16, 16)

    zd = {}
    select_whole(info, False)

    @pl.loop(0, chunks)
    def _(i):
        cols = pl.ds(pl.multiple_of(i * CHUNK, CHUNK), CHUNK)
        packed = dot(pick[...], tok[:, cols]).astype(BF16)
        slots[0, :, 0, :, cols] = packed[:64].reshape(2, 32, CHUNK)
        zst_a[:, :, :, cols] = packed[64:].reshape(7, 2, 32, CHUNK)

    for r in (2, 6, 4, 3, 7, 5, 1):
        zd[0, r] = remote(
            zst_a.at[r - 1], slots.at[0, :, r], sz.at[0, r], rz.at[0, r], at_z(r // 2, r % 2)
        )
        zd[0, r].start()

    for load in loads[:3]:
        load.wait()
    gate = dot(tok[...], sg[...])
    up = dot(tok[...], su[...])
    shid[...] = (silu(gate) * up).astype(BF16)

    @pl.loop(0, chunks)
    def _(i):
        cols = pl.ds(pl.multiple_of(i * CHUNK, CHUNK), CHUNK)
        acc[:, cols] = dot(shid[...], sd[:, cols])

    def pack_split(j):
        select_split(xinfo.at[j - 1], False)

        @pl.loop(0, chunks)
        def _(i):
            cols = pl.ds(pl.multiple_of(i * CHUNK, CHUNK), CHUNK)
            packed = dot(pick[:224, :], xbuf[j - 1, :, cols]).astype(BF16)
            slots[j, :, 0, :, cols] = packed[:64].reshape(2, 32, CHUNK)
            zst_s[j - 1, :, :, cols] = packed[64:128].reshape(2, 32, CHUNK)
            zst_b[j - 1, :, :, cols] = packed[128:224].reshape(6, 16, CHUNK)

        for r in (2, 6, 4, 3, 7, 5):
            zd[j, r] = remote(
                zst_b.at[j - 1, r - 2],
                slots.at[j, e_y, r, pl.ds(h_y, 16)],
                sz.at[j, r],
                rz.at[j, r],
                at_z(r // 2, r % 2),
            )
            zd[j, r].start()
        zd[j, 1] = remote(
            zst_s.at[j - 1], slots.at[j, :, 1], sz.at[j, 1], rz.at[j, 1], at_z(0, 1)
        )
        zd[j, 1].start()

    yd = {}

    def forward(j):
        for r in (2, 6, 4, 3, 7, 5):
            zd[j, r].wait_recv()
        mine = slots.at[j, e_y, pl.ds(2, 6), pl.ds(h_y, 16)]
        for p in (1, 3, 2):
            yd[j, p] = remote(mine, mine, sy.at[j, p], ry.at[j, p], at_y(p))
            yd[j, p].start()

    back = {}
    yb = {}

    def experts(j):
        if j == 0:
            for load in loads[3:]:
                load.wait()
            for r in range(2, 8):
                zd[j, r].wait_recv()
        else:
            for p in (1, 3, 2):
                yd[j, p].wait_recv()
                yd[j, p].wait_send()
        zd[j, 1].wait_recv()

        @pl.loop(0, 2)
        def _(e):
            given = slots[j, e].reshape(256, width)
            gate = dot(given, wg[e])
            up = dot(given, wu[e])
            hid[...] = (silu(gate) * up).astype(BF16)

            @pl.loop(0, chunks)
            def _(i):
                cols = pl.ds(pl.multiple_of(i * CHUNK, CHUNK), CHUNK)
                slots[j, e, :, :, cols] = (
                    dot(hid[...], wd[e, :, cols]).astype(BF16).reshape(8, 32, CHUNK)
                )

        if j in WHOLE:
            for r in (2, 6, 4, 3, 7, 5, 1):
                back[j, r] = remote(
                    slots.at[j, :, r],
                    zr_a.at[j, r],
                    szr.at[j, r],
                    rzr.at[j, r],
                    at_z(-(r // 2), r % 2),
                )
                back[j, r].start()
            zr_a[j, 0] = slots[j, :, 0]
        else:
            n = SPLIT.index(j)
            for p in (1, 3, 2):
                to = lax.rem(y + p, 4)
                yb[j, p] = remote(
                    slots.at[
                        j, lax.div(to, 2), pl.ds(2, 6), pl.ds(pl.multiple_of(lax.rem(to, 2) * 16, 16), 16)
                    ],
                    ybuf.at[n, p - 1],
                    syr.at[j, p],
                    ryr.at[j, p],
                    at_y(p),
                )
                yb[j, p].start()
            back[j, 1] = remote(
                slots.at[j, :, 1], zr_s.at[n, 1], szr.at[j, 1], rzr.at[j, 1], at_z(0, 1)
            )
            back[j, 1].start()
            zr_s[n, 0] = slots[j, :, 0]

    def sum_over_y(j):
        n = SPLIT.index(j)
        for p in (1, 3, 2):
            yb[j, p].wait_recv()

        @pl.loop(0, chunks)
        def _(i):
            cols = pl.ds(pl.multiple_of(i * CHUNK, CHUNK), CHUNK)
            total = slots[j, e_y, 2:8, pl.ds(h_y, 16), cols].astype(F32)
            for p in range(3):
                total = total + ybuf[n, p, :, :, cols].astype(F32)
            ysum[n, :, :, cols] = total.astype(BF16)

        for r in (2, 6, 4, 3, 7, 5):
            back[j, r] = remote(
                ysum.at[n, r - 2],
                zr_b.at[n, r - 2],
                szr.at[j, r],
                rzr.at[j, r],
                at_z(-(r // 2), r % 2),
            )
            back[j, r].start()

    def weigh(a, b):
        return lax.dot_general(a, b, (((0,), (0,)), ((), ())), preferred_element_type=F32)

    xd = {}

    def combine(j):
        table = info if j == 0 else xinfo.at[j - 1]
        if j in WHOLE:
            select_whole(table, True)
        else:
            select_split(table, True)
        for r in range(1, 8):
            back[j, r].wait_recv()
        if j == 1:
            relay[1].wait_send()
        if j == 3:
            relay[3].wait_send()

        @pl.loop(0, chunks)
        def _(i):
            cols = pl.ds(pl.multiple_of(i * CHUNK, CHUNK), CHUNK)
            if j in WHOLE:
                value = weigh(pick[...], zr_a[j, :, :, :, cols].reshape(512, CHUNK))
            else:
                n = SPLIT.index(j)
                value = weigh(pick[:128, :], zr_s[n, :, :, :, cols].reshape(128, CHUNK))
                value = value + weigh(pick[128:224, :], zr_b[n, :, :, cols].reshape(96, CHUNK))
            if j == 0:
                acc[:, cols] = acc[:, cols] + value
            else:
                xbuf[j - 1, :, cols] = value.astype(BF16)

        if j != 0:
            xd[j] = remote(xbuf.at[j - 1], xr.at[j - 1], sxr.at[j], rxr.at[j], at_x(j))
            xd[j].start()

    for j in (1, 3):
        near[j].wait_recv()
        relay[j].start()
        tell[j].wait_recv()
        pack_split(j)
    experts(0)
    forward(1)
    forward(3)
    relay[1].wait_recv()
    relay[3].wait_recv()
    tell[2].wait_recv()
    pack_split(2)
    experts(1)
    forward(2)
    experts(3)
    combine(0)
    combine(1)
    experts(2)
    sum_over_y(3)
    combine(3)
    sum_over_y(2)
    combine(2)

    for j in (1, 3, 2):
        xd[j].wait_recv()
    y2 = {}
    for p in (1, 3, 2):
        cols = pl.ds(pl.multiple_of(lax.rem(y + p, 4) * 512, 512), 512)
        total = acc[:, cols]
        for j in range(3):
            total = total + xr[j, :, cols].astype(F32)
        y2s[p - 1] = total.astype(BF16)
        y2[p] = remote(y2s.at[p - 1], y2r.at[p - 1], sy2.at[p], ry2.at[p], at_y(p))
        y2[p].start()
    cols = pl.ds(pl.multiple_of(y * 512, 512), 512)
    total = acc[:, cols]
    for j in range(3):
        total = total + xr[j, :, cols].astype(F32)
    acc[:, cols] = total
    for p in (1, 3, 2):
        y2[p].wait_recv()
    total = acc[:, cols]
    for p in range(3):
        total = total + y2r[p].astype(F32)
    out[...] = total.astype(BF16)

    for group in (near, tell):
        for copy in group.values():
            copy.wait_send()
    for group in (zd, back, yb, xd, y2):
        for copy in group.values():
            copy.wait_send()


def layer(tokens, routes, gates, w_gate, w_up, w_down, s_gate, s_up, s_down):
    rows, width = tokens.shape
    ff, sff = w_gate.shape[2], s_gate.shape[1]
    routes_t = jnp.pad(routes.T, ((0, 2), (0, 0)), constant_values=-1)
    gates_t = jnp.pad(gates.T, ((0, 2), (0, 0)))
    vmem = pl.BlockSpec(memory_space=pltpu.VMEM)
    hbm = pl.BlockSpec(memory_space=pl.ANY)
    dma = pltpu.SemaphoreType.DMA
    return pl.pallas_call(
        kernel,
        out_shape=jax.ShapeDtypeStruct((rows, width // 4), BF16),
        in_specs=[vmem] * 3 + [hbm] * 6,
        out_specs=vmem,
        scratch_shapes=[
            pltpu.VMEM((16, rows), F32),
            pltpu.VMEM((3, 16, rows), F32),
            pltpu.VMEM((3, rows, width), BF16),
            pltpu.VMEM((4, 2, 8, 32, width), BF16),
            pltpu.VMEM((7, 2, 32, width), BF16),
            pltpu.VMEM((3, 2, 32, width), BF16),
            pltpu.VMEM((3, 6, 16, width), BF16),
            pltpu.VMEM((2, 3, 6, 16, width), BF16),
            pltpu.VMEM((2, 6, 16, width), BF16),
            pltpu.VMEM((2, 8, 2, 32, width), BF16),
            pltpu.VMEM((2, 2, 2, 32, width), BF16),
            pltpu.VMEM((2, 6, 16, width), BF16),
            pltpu.VMEM((3, rows, width), BF16),
            pltpu.VMEM((rows, width), F32),
            pltpu.VMEM((3, rows, width // 4), BF16),
            pltpu.VMEM((3, rows, width // 4), BF16),
            pltpu.VMEM((512, rows), BF16),
            pltpu.VMEM((256, ff), BF16),
            pltpu.VMEM((rows, sff), BF16),
            pltpu.VMEM(w_gate.shape, BF16),
            pltpu.VMEM(w_up.shape, BF16),
            pltpu.VMEM(w_down.shape, BF16),
            pltpu.VMEM(s_gate.shape, BF16),
            pltpu.VMEM(s_up.shape, BF16),
            pltpu.VMEM(s_down.shape, BF16),
            dma((4,)), dma((4,)),
            dma((3,)), dma((3,)),
            dma((4, 8)), dma((4, 8)),
            dma((4, 4)), dma((4, 4)),
            dma((4, 8)), dma((4, 8)),
            dma((4, 4)), dma((4, 4)),
            dma((4,)), dma((4,)),
            dma((4,)), dma((4,)),
            dma((6,)),
        ],
        compiler_params=pltpu.CompilerParams(
            collective_id=0, has_side_effects=True, vmem_limit_bytes=67043328
        ),
    )(tokens, routes_t, gates_t, w_gate, w_up, w_down, s_gate, s_up, s_down)


def solution(mesh):
    placed = (
        P("dp", None),
        P("dp", None),
        P("dp", None),
        P("dp", None, "expert"),
        P("dp", None, "expert"),
        P("dp", "expert", None),
        P(None, "expert"),
        P(None, "expert"),
        P("expert", None),
    )
    return jax.shard_map(
        layer, mesh=mesh, in_specs=placed, out_specs=P("dp", "expert"), check_vma=False
    )
```

time: 282 us -> 202 us (0.72); the launches traced: 278 us -> 201 us
  Pallas kernels: 0 us -> 182 us
  blocking collectives: 111 us -> 0 us
  waiting for transfers between devices: 40.6 us -> 0 us
  matrix products: 37.3 us -> 0 us
  local copies, waits for them, and re-layouts: 52.3 us -> 19.4 us
  starting transfers between devices: 14.6 us -> 0 us
  between operations: 13.3 us -> 0.01 us
  other arithmetic: 8 us -> 0 us
    pallas_call x0 -> x1, Pallas kernels: none -> 182 us  [layer(): pl.pallas_call(kernel, out_shape=jax.ShapeDtypeStruct((rows, width // 4),...]
    all_to_all x2 -> x0, blocking collectives: 111 us -> none  [items_in_groups(): lax.all_to_all(group, axis, split_axis=split_dim, concat_axis=concat_dim,...]
    dot_general x7 -> x0, matrix products: 37.3 us -> none  [the longest x2 16.5 us: expert_work(): jnp.einsum('sjcf,jfd->sjcd', hidden, w_down, preferred_element_type=jnp.f...]
    gather x3 -> x0, local copies, waits for them, and re-layouts: 28.8 us -> none  [the longest x1 17.7 us: body(): outgoing = padded[sources].reshape(groups, local_experts, capacity, width)]
    reduce_scatter x3 -> x0, waiting for transfers between devices: 26.6 us -> none  [the longest x2 26.5 us: expert_work(): lax.psum_scatter(partial_value.astype(jnp.bfloat16), 'expert', scatter_di...]
    all_to_all x2 -> x0, starting transfers between devices: 14.5 us -> none  [expert_work(): return lax.all_to_all(summed, 'dp', split_axis=0, concat_axis=0, tiled=True)]
    all_to_all x2 -> x0, waiting for transfers between devices: 14 us -> none  [expert_work(): return lax.all_to_all(summed, 'dp', split_axis=0, concat_axis=0, tiled=True)]
    unnamed x13 -> x9, local copies, waits for them, and re-layouts: 4.09 us -> 16.8 us
  transfers between devices with their start and end apart: 5 -> 0, of which waited for: 2 -> 0; matrix products, arithmetic and copies ran while one was open for 16% -> 0% of each run, Pallas kernels for 0% -> 0%
where the time goes in v1:
time: 202 us; the launch traced here: 201 us
  Pallas kernels  182 us (90%)
  local copies, waits for them, and re-layouts  19.4 us (10%)
    pallas_call x1, Pallas kernels, layer(): pl.pallas_call(kernel, out_shape=jax.ShapeDtypeStruct((rows, width // 4),...  182 us
    unnamed x9, local copies, waits for them, and re-layouts  16.8 us

profile of v1, /device:TPU:2, one launch (start us, length us, event | category | flops | bytes accessed | tf_op | source)
XLA Modules:
  0.0 201.2 jit_solution(17973215773627323141)
XLA Ops:
  0.0 1.3 pad.8.routes_t
  1.3 1.3 pad.9.gates_t
  2.6 0.0 copy-start
  2.6 4.7 %copy.10.wg_h = bf16[2,2048,352]{2,1,0:T(8,128)(2,1)} copy(bf16[2,2048,352]{1,2,0:T(8,128)(2,1)} %param.12) | data formatting | bytes 5767168 | tf_op args[3]
  7.3 0.0 copy-done
  7.3 2.8 %copy.11.wu_h = bf16[2,2048,352]{2,1,0:T(8,128)(2,1)} copy(bf16[2,2048,352]{1,2,0:T(8,128)(2,1)S(1)} %copy-done) | data formatting | bytes 5767168 | tf_op args[4]
  10.1 0.0 copy-start.1
  10.1 4.8 %copy.12.sg_h = bf16[2048,704]{1,0:T(8,128)(2,1)} copy(bf16[2048,704]{0,1:T(8,128)(2,1)} %param.15) | data formatting | bytes 5767168 | tf_op args[6]
  14.9 0.0 copy-done.1
  14.9 2.8 %copy.13.su_h = bf16[2048,704]{1,0:T(8,128)(2,1)} copy(bf16[2048,704]{0,1:T(8,128)(2,1)S(1)} %copy-done.1) | data formatting | bytes 5767168 | tf_op args[7]
  17.8 181.7 %shard_map.91 = bf16[256,512]{1,0:T(8,128)(2,1)} custom-call(bf16[256,2048]{1,0:T(8,128)(2,1)} %tok.1, s32[8,256]{1,0:T(8,128)} %pad.8.routes_t, f32[8,256]{1,0:T(8,128)} %pad.9.gates_t, bf16[2,2048,352]{2,1,0:T(8,128)(2,1)} %copy.10.wg_h, bf16[2,2048,352]{2,1,0:T(8,128)(2,1)} %copy.11.wu_h, bf16[2,352,2048]{2,1,0:T(8,128)(2,1)} %wd_h.1, ...), custom_call_target="tpu_custom_call" | custom-call | tf_op jit(solution)/shard_map/pallas_call | solution.py:378
  199.5 1.7 copy.15
Async XLA Ops:
  2.6 4.7 %copy-start = (bf16[2,2048,352]{1,2,0:T(8,128)(2,1)S(1)}, bf16[2,2048,352]{1,2,0:T(8,128)(2,1)}, u32[]{:S(2)}) copy-start(bf16[2,2048,352]{1,2,0:T(8,128)(2,1)} %param.13) | copy-start | bytes 8650756
  10.1 4.8 %copy-start.1 = (bf16[2048,704]{0,1:T(8,128)(2,1)S(1)}, bf16[2048,704]{0,1:T(8,128)(2,1)}, u32[]{:S(2)}) copy-start(bf16[2048,704]{0,1:T(8,128)(2,1)} %param.16) | copy-start | bytes 8650756

commit v2 on v0

v2 whole, which is shorter than its diff:
```python
import jax
import jax.numpy as jnp
from jax import lax
from jax.experimental import pallas as pl
from jax.experimental.pallas import tpu as pltpu
from jax.sharding import PartitionSpec as P

MESH = pl.DeviceIdType.MESH
BF16 = jnp.bfloat16
F32 = jnp.float32
CAP = 32
CHUNK = 512
SENT = ((0, 1), (0, 1))
WHOLE = ((0, 1), (0, 3))
SPLIT = ((3, 2), (1, 2))
FAR = (2, 6, 4, 3, 7, 5)
SIDES = (0, 1)


def dot(a, b):
    return jnp.dot(a, b, preferred_element_type=F32)


def dot_t(a, b):
    return lax.dot_general(a, b, (((1,), (1,)), ((), ())), preferred_element_type=F32)


def silu(v):
    return v / (1.0 + jnp.exp(-v))


def kernel(
    tok, routes_t, gates_t, wg_h, wu_h, wd_h, sg_h, su_h, sd_h, out,
    info, xinfo, xbuf, slots, zst_a, zst_s, zst_b, ybuf_0, ybuf_1, ysum_0, ysum_1, zr_a, zr_s, zr_b, xr, acc, y2s, y2r,
    pick, weights, hid, shid, wg, wu, wd, sg, su, sd,
    sx, rx, si, ri, sz, rz, sy, ry, szr, rzr, syr, ryr, sxr, rxr, sy2, ry2, wsem,
):
    me = lax.axis_index("dp")
    y = lax.axis_index("expert")
    x = lax.div(me, 8)
    z = lax.rem(lax.div(me, 2), 4)
    c = lax.rem(me, 2)
    width = tok.shape[1]
    chunks = width // CHUNK
    side = width // 2
    strip = width // 8

    def core_of(cc):
        return c if cc == 0 else 1 - c

    def shifted(along_x, d, cc):
        if along_x:
            return lax.rem(x + d + 4, 4) * 8 + z * 2 + core_of(cc)
        return x * 8 + lax.rem(z + d + 4, 4) * 2 + core_of(cc)

    def gathered(s, d):
        return {"dp": shifted(s == 0, d, 0)}

    def across(s, d, cc):
        return {"dp": shifted(s == 1, d, cc)}

    def at_y(p):
        return {"expert": lax.rem(y + p, 4)}

    def remote(src, dst, s, r, where):
        return pltpu.make_async_remote_copy(
            src_ref=src, dst_ref=dst, send_sem=s, recv_sem=r, device_id=where, device_id_type=MESH
        )

    peers = [across(s, r // 2, r % 2) for s in SIDES for r in range(2, 8)]
    peers += [across(0, 0, 1)]
    peers += [at_y(p) for p in (1, 2, 3)]
    barrier = pltpu.get_barrier_semaphore()
    for peer in peers:
        pl.semaphore_signal(barrier, inc=1, device_id=peer, device_id_type=MESH)
    loads = [
        pltpu.make_async_copy(src, dst, wsem.at[i])
        for i, (src, dst) in enumerate(
            ((sg_h, sg), (su_h, su), (sd_h, sd), (wg_h, wg), (wu_h, wu), (wd_h, wd))
        )
    ]
    for load in loads:
        load.start()

    def half_of(s):
        return pl.ds(s * side, side)

    def piece(s, i):
        return pl.ds(pl.multiple_of(s * side + i * CHUNK, CHUNK), CHUNK)

    near, relay = {}, {}
    half = tok.shape[0] // 2
    for s in SIDES:
        cols = half_of(s)
        for n, (j, start) in enumerate(((1, 0), (3, half))):
            near[s, j] = remote(
                tok.at[:, cols], xbuf.at[j - 1, :, cols], sx.at[s, n], rx.at[s, n], gathered(s, -j)
            )
            relay[s, j] = remote(
                xbuf.at[j - 1, pl.ds(start, half), cols],
                xbuf.at[1, pl.ds(start, half), cols],
                sx.at[s, 2 + n],
                rx.at[s, 2 + n],
                gathered(s, -j),
            )
    rt = routes_t[...]
    rows = tok.shape[0]
    label = lax.broadcasted_iota(jnp.int32, (64, rows), 0)
    hits = jnp.zeros((64, rows), F32)
    for k in range(6):
        hits = hits + jnp.where(rt[k : k + 1, :] == label, 1.0, 0.0)
    earlier = jnp.where(
        lax.broadcasted_iota(jnp.int32, (rows, rows), 0)
        < lax.broadcasted_iota(jnp.int32, (rows, rows), 1),
        1.0,
        0.0,
    )
    before = dot(hits.astype(BF16), earlier.astype(BF16))
    info[...] = jnp.full(info.shape, -1.0, F32)
    for k in range(6):
        slot = jnp.sum(jnp.where(rt[k : k + 1, :] == label, before, 0.0), axis=0, keepdims=True)
        info[k : k + 1, :] = rt[k : k + 1, :].astype(F32) * CAP + slot
        info[8 + k : 9 + k, :] = gates_t[k : k + 1, :]
    tell = {}
    for j in (1, 3, 2):
        for s in SIDES:
            tell[s, j] = remote(
                info, xinfo.at[s * 3 + j - 1], si.at[s, j - 1], ri.at[s, j - 1], gathered(s, -j)
            )

    def base_of(s, r):
        return shifted(s == 1, r // 2, r % 2) * 64

    def place(s, j, r):
        if s == 0:
            return j, r
        return (4 - r // 2) % 4, 2 * ((4 - j) % 4) + r % 2

    def select(into, table, base, count, at, weighted):
        ids = (lax.broadcasted_iota(jnp.int32, (count, rows), 0) + base).astype(F32)
        value = jnp.zeros((count, rows), F32)
        for k in range(6):
            given = table[8 + k : 9 + k, :] if weighted else 1.0
            value = value + jnp.where(ids == table[k : k + 1, :], given, 0.0)
        into[at : at + count, :] = value.astype(BF16)

    def select_whole(into, table, s, weighted):
        for r in range(8):
            select(into, table, base_of(s, r), 64, r * 64, weighted)

    def select_split(into, table, s, weighted):
        for r in range(2):
            select(into, table, base_of(s, r), 64, r * 64, weighted)
        for r in range(2, 8):
            select(into, table, base_of(s, r) + 16 * y, 16, 128 + (r - 2) * 16, weighted)

    e_y, h_y = lax.div(y, 2), pl.multiple_of(lax.rem(y, 2) * 16, 16)

    zd = {}

    def pack(s, j):
        table = info if j == 0 else xinfo.at[s * 3 + j - 1]
        source = tok if j == 0 else xbuf.at[j - 1]
        mine, row = place(s, j, 0)
        split = j in SENT[s]
        if split:
            n = SENT[s].index(j)
            select_split(pick, table, s, False)
        else:
            n = 0 if j == 3 else 1
            select_whole(pick, table, s, False)

        @pl.loop(0, 2)
        def _(i):
            cols = piece(s, i)
            if split:
                packed = dot(pick[:224, :], source[:, cols]).astype(BF16)
                zst_s[n, :, :, cols] = packed[64:128].reshape(2, 32, CHUNK)
                zst_b[n, :, :, cols] = packed[128:224].reshape(6, 16, CHUNK)
            else:
                packed = dot(pick[...], source[:, cols]).astype(BF16)
                zst_a[n, :, :, :, cols] = packed[64:].reshape(7, 2, 32, CHUNK)
            slots[mine, :, row, :, cols] = packed[:64].reshape(2, 32, CHUNK)

    def send(s, j):
        table = info if j == 0 else xinfo.at[s * 3 + j - 1]
        split = j in SENT[s]
        n = SENT[s].index(j) if split else (0 if j == 3 else 1)
        cols = half_of(s)
        for r in FAR + (1,):
            block, to = place(s, j, r)
            whole = slots.at[block, :, to, :, cols]
            if not split:
                source, target = zst_a.at[n, r - 1, :, :, cols], whole
            elif r == 1:
                source, target = zst_s.at[n, :, :, cols], whole
            else:
                source = zst_b.at[n, r - 2, :, cols]
                target = slots.at[block, e_y, to, pl.ds(h_y, 16), cols]
            zd[s, j, r] = remote(
                source, target, sz.at[s, j, r - 1], rz.at[s, j, r - 1], across(s, r // 2, r % 2)
            )
            zd[s, j, r].start()
        if j in WHOLE[s]:
            select_whole(weights.at[s * 4 + j], table, s, True)
        else:
            select_split(weights.at[s * 4 + j], table, s, True)

    def shared():
        for load in loads[:3]:
            load.wait()
        gate = dot_t(tok[...], sg[...])
        up = dot_t(tok[...], su[...])
        shid[...] = (silu(gate) * up).astype(BF16)
        for h in SIDES:

            @pl.loop(0, 4)
            def _(i):
                given = pl.ds(pl.multiple_of(i * 2 * strip + h * strip, strip), strip)
                put = pl.ds(pl.multiple_of(h * side + i * strip, strip), strip)
                acc[:, put] = dot(shid[...], sd[:, given])

    yd = {}

    def forward(s, j):
        for r in FAR:
            zd[s, j, r].wait_recv()
        if s == 0:
            mine = slots.at[j, e_y, pl.ds(2, 6), pl.ds(h_y, 16), half_of(s)]
        else:
            row = place(s, j, 0)[1]
            mine = slots.at[pl.ds(1, 3), e_y, pl.ds(row, 2), pl.ds(h_y, 16), half_of(s)]
        for p in (1, 3, 2):
            yd[s, j, p] = remote(mine, mine, sy.at[s, j, p - 1], ry.at[s, j, p - 1], at_y(p))
            yd[s, j, p].start()

    back = {}
    yb = {}
    shared_on = set()

    def arrived(b):
        d = (4 - b) % 4
        if b in SENT[0]:
            sent = [(0, b)]
        else:
            sent = []
            for r in FAR:
                zd[0, b, r].wait_recv()
        zd[0, b, 1].wait_recv()
        for j in range(4):
            if d == 0:
                zd[1, j, 1].wait_recv()
            elif j in SENT[1]:
                sent.append((1, j))
            else:
                for r in (2 * d, 2 * d + 1):
                    zd[1, j, r].wait_recv()
        for s, j in sent:
            if (s, j) not in shared_on:
                shared_on.add((s, j))
                for p in (1, 3, 2):
                    yd[s, j, p].wait_recv()
                    yd[s, j, p].wait_send()

    def give_back(s, j, r, source, target):
        back[s, j, r] = remote(
            source, target, szr.at[s, j, r - 1], rzr.at[s, j, r - 1], across(s, -(r // 2), r % 2)
        )
        back[s, j, r].start()

    def give_to_y(s, b, rows_at, rows_n, target):
        for p in (1, 3, 2):
            to = lax.rem(y + p, 4)
            first = pl.multiple_of(lax.rem(to, 2) * 16, 16)
            yb[s, b, p] = remote(
                slots.at[b, lax.div(to, 2), pl.ds(rows_at, rows_n), pl.ds(first, 16), half_of(s)],
                target.at[p - 1],
                syr.at[s * 2 + b - 1 - (s == 0), p - 1],
                ryr.at[s * 2 + b - 1 - (s == 0), p - 1],
                at_y(p),
            )
            yb[s, b, p].start()

    def give_whole(b):
        n, cols = WHOLE[0].index(b), half_of(0)
        for r in FAR + (1,):
            give_back(0, b, r, slots.at[b, :, r, :, cols], zr_a.at[n, r, :, :, cols])

    def experts(b):
        arrived(b)

        @pl.loop(0, 2)
        def _(e):
            given = slots[b, e].reshape(256, width)
            gate = dot_t(given, wg[e])
            up = dot_t(given, wu[e])
            hid[e] = (silu(gate) * up).astype(BF16)

        for s in (1, 0):

            @pl.loop(0, 4)
            def _(i):
                given = pl.ds(pl.multiple_of(i * 2 * strip + s * strip, strip), strip)
                put = pl.ds(pl.multiple_of(s * side + i * strip, strip), strip)
                for e in range(2):
                    value = dot(hid[e], wd[e, :, given]).astype(BF16)
                    slots[b, e, :, :, put] = value.reshape(8, 32, strip)

            cols = half_of(s)
            d = (4 - b) % 4
            if s == 0:
                if b in WHOLE[0]:
                    n = WHOLE[0].index(b)
                    if b != 0:
                        give_whole(b)
                    zr_a[n, 0, :, :, cols] = slots[b, :, 0, :, cols]
                else:
                    n = SPLIT[0].index(b)
                    give_to_y(0, b, 2, 6, ybuf_0.at[n])
                    give_back(0, b, 1, slots.at[b, :, 1, :, cols], zr_s.at[n, 1, :, :, cols])
                    zr_s[n, 0, :, :, cols] = slots[b, :, 0, :, cols]
                continue
            if d != 0:
                give_to_y(1, b, 4, 4, ybuf_1.at[b - 1])
            for j in (3, 0, 1, 2):
                row = 2 * ((4 - j) % 4)
                if j in WHOLE[1]:
                    n, into = WHOLE[1].index(j), zr_a
                else:
                    n, into = SPLIT[1].index(j), zr_s
                if d == 0:
                    into[n, 0, :, :, cols] = slots[b, :, row, :, cols]
                    give_back(1, j, 1, slots.at[b, :, row + 1, :, cols], into.at[n, 1, :, :, cols])
                elif j in WHOLE[1]:
                    for cc in range(2):
                        give_back(
                            1,
                            j,
                            2 * d + cc,
                            slots.at[b, :, row + cc, :, cols],
                            zr_a.at[n, 2 * d + cc, :, :, cols],
                        )

    def sum_over_y(s, b):
        for p in (1, 3, 2):
            yb[s, b, p].wait_recv()
        if s == 0:
            n = SPLIT[0].index(b)
            rows_at, parts, into = 2, ybuf_0.at[n], ysum_0.at[n]
        else:
            rows_at, parts, into = 4, ybuf_1.at[b - 1], ysum_1.at[b - 1]
        for i in range(2):
            cols = pl.ds(i * CHUNK, CHUNK)
            total = slots[
                b, e_y, rows_at:8, pl.ds(h_y, 16), pl.ds(s * side + i * CHUNK, CHUNK)
            ].astype(F32)
            for p in range(3):
                total = total + parts[p, :, :, cols].astype(F32)
            into[:, :, cols] = total.astype(BF16)

        for row in range(rows_at, 8):
            if s == 0:
                j, r = b, row
            else:
                j, r = (4 - row // 2) % 4, 2 * ((4 - b) % 4) + row % 2
            give_back(
                s, j, r, into.at[row - rows_at], zr_b.at[SPLIT[s].index(j), r - 2, :, half_of(s)]
            )

    def weigh(a, b):
        return lax.dot_general(a, b, (((0,), (0,)), ((), ())), preferred_element_type=F32)

    xd = {}

    def combine(s, j):
        for r in range(1, 8):
            back[s, j, r].wait_recv()
        if (s, j) in relay:
            relay[s, j].wait_send()

        @pl.loop(0, 2)
        def _(i):
            cols = piece(s, i)
            if j in WHOLE[s]:
                n = WHOLE[s].index(j)
                value = weigh(weights[s * 4 + j], zr_a[n, :, :, :, cols].reshape(512, CHUNK))
            else:
                n = SPLIT[s].index(j)
                value = weigh(
                    weights[s * 4 + j, :128, :], zr_s[n, :, :, :, cols].reshape(128, CHUNK)
                )
                value = value + weigh(
                    weights[s * 4 + j, 128:224, :], zr_b[n, :, :, cols].reshape(96, CHUNK)
                )
            if j == 0:
                acc[:, cols] = acc[:, cols] + value
            else:
                xbuf[j - 1, :, cols] = value.astype(BF16)

        if j != 0:
            cols = half_of(s)
            xd[s, j] = remote(
                xbuf.at[j - 1, :, cols],
                xr.at[j - 1, :, cols],
                sxr.at[s, j - 1],
                rxr.at[s, j - 1],
                gathered(s, j),
            )
            xd[s, j].start()

    y2 = {}

    def finish(h):
        for j in (1, 3, 2):
            xd[h, j].wait_recv()
        part = pl.ds(h * strip, strip)
        for p in (1, 3, 2, 0):
            cols = pl.ds(pl.multiple_of(h * side + lax.rem(y + p, 4) * strip, strip), strip)
            total = acc[:, cols]
            for j in range(3):
                total = total + xr[j, :, cols].astype(F32)
            if p == 0:
                acc[:, cols] = total
                continue
            y2s[p - 1, :, part] = total.astype(BF16)
            y2[h, p] = remote(
                y2s.at[p - 1, :, part], y2r.at[p - 1, :, part], sy2.at[h, p - 1], ry2.at[h, p - 1], at_y(p)
            )
            y2[h, p].start()

    for s in SIDES:
        pack(s, 0)
    pl.semaphore_wait(barrier, len(peers))
    for j in (1, 3, 2):
        for s in SIDES:
            tell[s, j].start()
    for s in SIDES:
        send(s, 0)
    for j in (1, 3):
        for s in SIDES:
            near[s, j].start()
    shared()
    for s in SIDES:
        forward(s, 0)
    for j in (1, 3):
        for s in SIDES:
            near[s, j].wait_recv()
            relay[s, j].start()
        for s in SIDES:
            tell[s, j].wait_recv()
            pack(s, j)
            send(s, j)
    for s in SIDES:
        forward(s, 1)
    for load in loads[3:]:
        load.wait()
    for s in SIDES:
        relay[s, 1].wait_recv()
        relay[s, 3].wait_recv()
        tell[s, 2].wait_recv()
        pack(s, 2)
        send(s, 2)
    experts(0)
    experts(1)
    give_whole(0)
    experts(3)
    experts(2)
    sum_over_y(1, 1)
    sum_over_y(1, 3)
    sum_over_y(0, 3)
    sum_over_y(1, 2)
    combine(0, 1)
    combine(1, 3)
    combine(0, 3)
    combine(1, 1)
    sum_over_y(0, 2)
    combine(0, 0)
    combine(1, 0)
    combine(0, 2)
    combine(1, 2)
    finish(0)
    finish(1)
    def write_out(h):
        part = pl.ds(h * strip, strip)
        for p in (1, 3, 2):
            y2[h, p].wait_recv()
        total = acc[:, pl.ds(pl.multiple_of(h * side + y * strip, strip), strip)]
        for p in range(3):
            total = total + y2r[p, :, part].astype(F32)
        out[:, part] = total.astype(BF16)

    def drain():
        for group in (near, tell, zd, back, yb, xd, y2):
            for copy in group.values():
                copy.wait_send()

    write_out(0)
    write_out(1)
    drain()


def layer(tokens, routes, gates, w_gate, w_up, w_down, s_gate, s_up, s_down):
    rows, width = tokens.shape
    ff, sff = w_gate.shape[2], s_gate.shape[1]
    gate_t, up_t = jnp.swapaxes(w_gate, 1, 2), jnp.swapaxes(w_up, 1, 2)
    vmem = pl.BlockSpec(memory_space=pltpu.VMEM)
    hbm = pl.BlockSpec(memory_space=pl.ANY)
    dma = pltpu.SemaphoreType.DMA
    return pl.pallas_call(
        kernel,
        out_shape=jax.ShapeDtypeStruct((rows, width // 4), BF16),
        in_specs=[vmem] * 3 + [hbm] * 6,
        out_specs=vmem,
        scratch_shapes=[
            pltpu.VMEM((16, rows), F32),
            pltpu.VMEM((6, 16, rows), F32),
            pltpu.VMEM((3, rows, width), BF16),
            pltpu.VMEM((4, 2, 8, 32, width), BF16),
            pltpu.VMEM((2, 7, 2, 32, width), BF16),
            pltpu.VMEM((2, 2, 32, width), BF16),
            pltpu.VMEM((2, 6, 16, width), BF16),
            pltpu.VMEM((2, 3, 6, 16, width // 2), BF16),
            pltpu.VMEM((3, 3, 4, 16, width // 2), BF16),
            pltpu.VMEM((2, 6, 16, width // 2), BF16),
            pltpu.VMEM((3, 4, 16, width // 2), BF16),
            pltpu.VMEM((2, 8, 2, 32, width), BF16),
            pltpu.VMEM((2, 2, 2, 32, width), BF16),
            pltpu.VMEM((2, 6, 16, width), BF16),
            pltpu.VMEM((3, rows, width), BF16),
            pltpu.VMEM((rows, width), F32),
            pltpu.VMEM((3, rows, width // 4), BF16),
            pltpu.VMEM((3, rows, width // 4), BF16),
            pltpu.VMEM((512, rows), BF16),
            pltpu.VMEM((8, 512, rows), BF16),
            pltpu.VMEM((2, 256, ff), BF16),
            pltpu.VMEM((rows, sff), BF16),
            pltpu.VMEM(gate_t.shape, BF16),
            pltpu.VMEM(up_t.shape, BF16),
            pltpu.VMEM(w_down.shape, BF16),
            pltpu.VMEM((sff, width), BF16),
            pltpu.VMEM((sff, width), BF16),
            pltpu.VMEM(s_down.shape, BF16),
            dma((2, 4)), dma((2, 4)),
            dma((2, 3)), dma((2, 3)),
            dma((2, 4, 7)), dma((2, 4, 7)),
            dma((2, 2, 3)), dma((2, 2, 3)),
            dma((2, 4, 7)), dma((2, 4, 7)),
            dma((5, 3)), dma((5, 3)),
            dma((2, 3)), dma((2, 3)),
            dma((2, 3)), dma((2, 3)),
            dma((6,)),
        ],
        compiler_params=pltpu.CompilerParams(
            collective_id=0, has_side_effects=True, vmem_limit_bytes=67043328
        ),
    )(tokens, routes.T, gates.T, gate_t, up_t, w_down, s_gate.T, s_up.T, s_down)


def solution(mesh):
    placed = (
        P("dp", None),
        P("dp", None),
        P("dp", None),
        P("dp", None, "expert"),
        P("dp", None, "expert"),
        P("dp", "expert", None),
        P(None, "expert"),
        P(None, "expert"),
        P("expert", None),
    )
    return jax.shard_map(
        layer, mesh=mesh, in_specs=placed, out_specs=P("dp", "expert"), check_vma=False
    )
```

time: 282 us -> 145 us (0.51); the launches traced: 278 us -> 145 us
  Pallas kernels: 0 us -> 143 us
  blocking collectives: 111 us -> 0 us
  local copies, waits for them, and re-layouts: 52.3 us -> 1.67 us
  waiting for transfers between devices: 40.6 us -> 0 us
  matrix products: 37.3 us -> 0 us
  starting transfers between devices: 14.6 us -> 0 us
  between operations: 13.3 us -> 0.01 us
  other arithmetic: 8 us -> 0 us
    pallas_call x0 -> x1, Pallas kernels: none -> 143 us  [layer(): pl.pallas_call(kernel, out_shape=jax.ShapeDtypeStruct((rows, width // 4),...]
    all_to_all x2 -> x0, blocking collectives: 111 us -> none  [items_in_groups(): lax.all_to_all(group, axis, split_axis=split_dim, concat_axis=concat_dim,...]
    dot_general x7 -> x0, matrix products: 37.3 us -> none  [the longest x2 16.5 us: expert_work(): jnp.einsum('sjcf,jfd->sjcd', hidden, w_down, preferred_element_type=jnp.f...]
    gather x3 -> x0, local copies, waits for them, and re-layouts: 28.8 us -> none  [the longest x1 17.7 us: body(): outgoing = padded[sources].reshape(groups, local_experts, capacity, width)]
    reduce_scatter x3 -> x0, waiting for transfers between devices: 26.6 us -> none  [the longest x2 26.5 us: expert_work(): lax.psum_scatter(partial_value.astype(jnp.bfloat16), 'expert', scatter_di...]
    all_to_all x2 -> x0, starting transfers between devices: 14.5 us -> none  [expert_work(): return lax.all_to_all(summed, 'dp', split_axis=0, concat_axis=0, tiled=True)]
    all_to_all x2 -> x0, waiting for transfers between devices: 14 us -> none  [expert_work(): return lax.all_to_all(summed, 'dp', split_axis=0, concat_axis=0, tiled=True)]
    scatter x1 -> x0, local copies, waits for them, and re-layouts: 6.18 us -> none  [body(): jnp.full((experts_all * capacity,), tok_rows, jnp.int32)]
  transfers between devices with their start and end apart: 5 -> 0, of which waited for: 2 -> 0; matrix products, arithmetic and copies ran while one was open for 16% -> 0% of each run, Pallas kernels for 0% -> 0%
where the time goes in v2:
time: 145 us
  Pallas kernels  143 us (99%)
  local copies, waits for them, and re-layouts  1.67 us (1%)
    pallas_call x1, Pallas kernels, layer(): pl.pallas_call(kernel, out_shape=jax.ShapeDtypeStruct((rows, width // 4),...  143 us

profile of v2, /device:TPU:2, one launch (start us, length us, event | category | flops | bytes accessed | tf_op | source)
XLA Modules:
  0.0 144.8 jit_solution(14468672670789511787)
XLA Ops:
  0.0 143.1 %shard_map.91 = bf16[256,512]{1,0:T(8,128)(2,1)} custom-call(bf16[256,2048]{1,0:T(8,128)(2,1)} %tok.1, s32[6,256]{1,0:T(8,128)} %bitcast.10, f32[6,256]{1,0:T(8,128)} %bitcast.11, bf16[2,352,2048]{2,1,0:T(8,128)(2,1)} %bitcast.6, bf16[2,352,2048]{2,1,0:T(8,128)(2,1)} %bitcast.7, bf16[2,352,2048]{2,1,0:T(8,128)(2,1)} %wd_h.1, bf16[704,2048]{1,0:T(8,128)(2,1)} %bitcast.8, ...), custom_call_target="tpu_custom_call" | custom-call | tf_op jit(solution)/shard_map/pallas_call | solution.py:509
  143.2 1.7 %copy.11 = bf16[256,512]{1,0:T(8,128)(2,1)} copy(bf16[256,512]{1,0:T(8,128)(2,1)} %shard_map.91) | data formatting | bytes 524288

commit v3 on v2

--- a/solution.py
+++ b/solution.py
@@ -11,9 +11,10 @@
 CAP = 32
 CHUNK = 512
 SENT = ((0, 1), (0, 1))
-WHOLE = ((0, 1), (0, 3))
-SPLIT = ((3, 2), (1, 2))
+WHOLE = ((0, 2), (0, 2))
+SPLIT = ((1, 3), (1, 3))
 FAR = (2, 6, 4, 3, 7, 5)
+PAIRS = (2, 6)
 SIDES = (0, 1)
 
 
@@ -268,18 +269,19 @@
         )
         back[s, j, r].start()
 
-    def give_to_y(s, b, rows_at, rows_n, target):
+    def give_to_y(s, b, part, rows_at, rows_n, target):
+        which = b // 2 if s == 0 else 2 * b + part
         for p in (1, 3, 2):
             to = lax.rem(y + p, 4)
             first = pl.multiple_of(lax.rem(to, 2) * 16, 16)
-            yb[s, b, p] = remote(
+            yb[s, b, part, p] = remote(
                 slots.at[b, lax.div(to, 2), pl.ds(rows_at, rows_n), pl.ds(first, 16), half_of(s)],
                 target.at[p - 1],
-                syr.at[s * 2 + b - 1 - (s == 0), p - 1],
-                ryr.at[s * 2 + b - 1 - (s == 0), p - 1],
+                syr.at[which, p - 1],
+                ryr.at[which, p - 1],
                 at_y(p),
             )
-            yb[s, b, p].start()
+            yb[s, b, part, p].start()
 
     def give_whole(b):
         n, cols = WHOLE[0].index(b), half_of(0)
@@ -311,18 +313,18 @@
             if s == 0:
                 if b in WHOLE[0]:
                     n = WHOLE[0].index(b)
-                    if b != 0:
-                        give_whole(b)
+                    give_whole(b)
                     zr_a[n, 0, :, :, cols] = slots[b, :, 0, :, cols]
                 else:
                     n = SPLIT[0].index(b)
-                    give_to_y(0, b, 2, 6, ybuf_0.at[n])
+                    give_to_y(0, b, 0, 2, 6, ybuf_0.at[n])
                     give_back(0, b, 1, slots.at[b, :, 1, :, cols], zr_s.at[n, 1, :, :, cols])
                     zr_s[n, 0, :, :, cols] = slots[b, :, 0, :, cols]
                 continue
             if d != 0:
-                give_to_y(1, b, 4, 4, ybuf_1.at[b - 1])
-            for j in (3, 0, 1, 2):
+                for part in range(2):
+                    give_to_y(1, b, part, PAIRS[part], 2, ybuf_1.at[b - 1, part])
+            for j in (2, 0, 1, 3):
                 row = 2 * ((4 - j) % 4)
                 if j in WHOLE[1]:
                     n, into = WHOLE[1].index(j), zr_a
@@ -342,30 +344,41 @@
                         )
 
     def sum_over_y(s, b):
-        for p in (1, 3, 2):
-            yb[s, b, p].wait_recv()
         if s == 0:
             n = SPLIT[0].index(b)
-            rows_at, parts, into = 2, ybuf_0.at[n], ysum_0.at[n]
+            groups = ((0, 2, 6, ybuf_0.at[n], ysum_0.at[n]),)
         else:
-            rows_at, parts, into = 4, ybuf_1.at[b - 1], ysum_1.at[b - 1]
-        for i in range(2):
-            cols = pl.ds(i * CHUNK, CHUNK)
-            total = slots[
-                b, e_y, rows_at:8, pl.ds(h_y, 16), pl.ds(s * side + i * CHUNK, CHUNK)
-            ].astype(F32)
-            for p in range(3):
-                total = total + parts[p, :, :, cols].astype(F32)
-            into[:, :, cols] = total.astype(BF16)
-
-        for row in range(rows_at, 8):
-            if s == 0:
-                j, r = b, row
-            else:
-                j, r = (4 - row // 2) % 4, 2 * ((4 - b) % 4) + row % 2
-            give_back(
-                s, j, r, into.at[row - rows_at], zr_b.at[SPLIT[s].index(j), r - 2, :, half_of(s)]
-            )
+            groups = tuple(
+                (part, PAIRS[part], 2, ybuf_1.at[b - 1, part], ysum_1.at[b - 1, part])
+                for part in range(2)
+            )
+        for part, rows_at, count, parts, into in groups:
+            for p in (1, 3, 2):
+                yb[s, b, part, p].wait_recv()
+            for i in range(2):
+                cols = pl.ds(i * CHUNK, CHUNK)
+                total = slots[
+                    b,
+                    e_y,
+                    rows_at : rows_at + count,
+                    pl.ds(h_y, 16),
+                    pl.ds(s * side + i * CHUNK, CHUNK),
+                ].astype(F32)
+                for p in range(3):
+                    total = total + parts[p, :, :, cols].astype(F32)
+                into[:, :, cols] = total.astype(BF16)
+            for row in range(rows_at, rows_at + count):
+                if s == 0:
+                    j, r = b, row
+                else:
+                    j, r = (4 - row // 2) % 4, 2 * ((4 - b) % 4) + row % 2
+                give_back(
+                    s,
+                    j,
+                    r,
+                    into.at[row - rows_at],
+                    zr_b.at[SPLIT[s].index(j), r - 2, :, half_of(s)],
+                )
 
     def weigh(a, b):
         return lax.dot_general(a, b, (((0,), (0,)), ((), ())), preferred_element_type=F32)
@@ -462,22 +475,21 @@
         send(s, 2)
     experts(0)
     experts(1)
-    give_whole(0)
+    experts(2)
     experts(3)
-    experts(2)
     sum_over_y(1, 1)
+    sum_over_y(0, 1)
+    combine(0, 2)
+    sum_over_y(1, 2)
+    combine(1, 2)
     sum_over_y(1, 3)
+    combine(0, 1)
     sum_over_y(0, 3)
-    sum_over_y(1, 2)
-    combine(0, 1)
-    combine(1, 3)
+    combine(0, 0)
+    combine(1, 0)
     combine(0, 3)
     combine(1, 1)
-    sum_over_y(0, 2)
-    combine(0, 0)
-    combine(1, 0)
-    combine(0, 2)
-    combine(1, 2)
+    combine(1, 3)
     finish(0)
     finish(1)
     def write_out(h):
@@ -520,9 +532,9 @@
             pltpu.VMEM((2, 2, 32, width), BF16),
             pltpu.VMEM((2, 6, 16, width), BF16),
             pltpu.VMEM((2, 3, 6, 16, width // 2), BF16),
-            pltpu.VMEM((3, 3, 4, 16, width // 2), BF16),
+            pltpu.VMEM((3, 2, 3, 2, 16, width // 2), BF16),
             pltpu.VMEM((2, 6, 16, width // 2), BF16),
-            pltpu.VMEM((3, 4, 16, width // 2), BF16),
+            pltpu.VMEM((3, 2, 2, 16, width // 2), BF16),
             pltpu.VMEM((2, 8, 2, 32, width), BF16),
             pltpu.VMEM((2, 2, 2, 32, width), BF16),
             pltpu.VMEM((2, 6, 16, width), BF16),
@@ -545,7 +557,7 @@
             dma((2, 4, 7)), dma((2, 4, 7)),
             dma((2, 2, 3)), dma((2, 2, 3)),
             dma((2, 4, 7)), dma((2, 4, 7)),
-            dma((5, 3)), dma((5, 3)),
+            dma((8, 3)), dma((8, 3)),
             dma((2, 3)), dma((2, 3)),
             dma((2, 3)), dma((2, 3)),
             dma((6,)),

time: 145 us -> 135 us (0.931)
  Pallas kernels: 143 us -> 133 us
    pallas_call x1, Pallas kernels: 143 us -> 133 us  [layer(): pl.pallas_call(kernel, out_shape=jax.ShapeDtypeStruct((rows, width // 4),...]
where the time goes in v3:
time: 135 us
  Pallas kernels  133 us (99%)
  local copies, waits for them, and re-layouts  1.67 us (1%)
    pallas_call x1, Pallas kernels, layer(): pl.pallas_call(kernel, out_shape=jax.ShapeDtypeStruct((rows, width // 4),...  133 us

profile of v3, /device:TPU:2, one launch (start us, length us, event | category | flops | bytes accessed | tf_op | source)
XLA Modules:
  0.0 134.8 jit_solution(17815744503792144792)
XLA Ops:
  0.0 133.1 %shard_map.91 = bf16[256,512]{1,0:T(8,128)(2,1)} custom-call(bf16[256,2048]{1,0:T(8,128)(2,1)} %tok.1, s32[6,256]{1,0:T(8,128)} %bitcast.10, f32[6,256]{1,0:T(8,128)} %bitcast.11, bf16[2,352,2048]{2,1,0:T(8,128)(2,1)} %bitcast.6, bf16[2,352,2048]{2,1,0:T(8,128)(2,1)} %bitcast.7, bf16[2,352,2048]{2,1,0:T(8,128)(2,1)} %wd_h.1, bf16[704,2048]{1,0:T(8,128)(2,1)} %bitcast.8, ...), custom_call_target="tpu_custom_call" | custom-call | tf_op jit(solution)/shard_map/pallas_call | solution.py:521
  133.2 1.7 %copy.11 = bf16[256,512]{1,0:T(8,128)(2,1)} copy(bf16[256,512]{1,0:T(8,128)(2,1)} %shard_map.91) | data formatting | bytes 524288
